TPU v7x, 32 devices: a whole 2x2x4 slice. The times are simulated.
32 devices in a mesh: groups: 2 (over y), ctx: 4 (over z), head: 2 (over x), rep: 2 (over core).
Axes of the slice: x: 2, y: 2, z: 4, core: 2. Of those that a mesh axis runs over, the one named last changes fastest.
Arguments:
- kv_cache: bfloat16 [4, 96, 128, 576], P(('groups', 'rep'), 'ctx'), parts along dimension 0, may hold values from -10 to 10
- queries: bfloat16 [4, 4, 128, 576], P(('groups', 'rep'), None, 'head'), parts along dimension 0, may hold values from -45 to 45
- new_latent: bfloat16 [4, 4, 576], P(('groups', 'rep')), parts along dimension 0, may hold values from -6 to 6
- page_counts: int32 [4, 4], P(('groups', 'rep')), parts along dimension 0, may hold values from 1 to 36, 72 in all within a row
- page_tails: int32 [4, 4], P(('groups', 'rep')), parts along dimension 0, may hold values from 1 to 128
- page_slots: int32 [4, 96], P(('groups', 'rep')), parts along dimension 0, may hold values from 0 to 95, each once within a row
Outputs:
- attended: bfloat16 [4, 4, 128, 512], P(('groups', 'rep'), None, 'head'), parts along dimension 0
There are 2 independent parts, one for each index of `groups`. A program takes and returns all parts, laid end to end along the dimension named above; each array names one. Nothing has to cross between parts.
Inputs may be any that keep to these rules, and one draw needn't show every extreme that they name: `page_counts`: the 4 counts of a half sum to 72, and the largest is exactly 36. `page_slots`: each half's row holds every slot once; only its first 72 entries are pages in use.
All inputs are finite; a program needn't handle non-finite values.
Results may differ from a plain program's by a relative error of at most 0.0033.
Values sent between devices are 32-bit elements; how exact they have to be, the bound alone decides.
A program may use at most 64 MiB of HBM per device.

v0:
```python
import functools
import math

import jax
import jax.numpy as jnp
from jax import lax
from jax.experimental import pallas as pl
from jax.experimental.pallas import tpu as pltpu
from jax.sharding import PartitionSpec as P

LATENT = 512
SCALE = 192.0 ** (-0.5) * math.log2(math.e)
NEG = -1e30
PIECES = 4
LAG = 6
MESH = pl.DeviceIdType.MESH


def kernel(
    n,
    counts_ref,
    tails_ref,
    slots_ref,
    latent_ref,
    q_hbm,
    kv_hbm,
    out_ref,
    q_v,
    kv_v,
    own_v,
    bias_v,
    score_v,
    weight_v,
    acc_v,
    inbox,
    part_v,
    cross,
    total_v,
    final,
    stat_out,
    stat_in,
    load_sem,
    stat_send,
    stat_recv,
    in_send,
    in_recv,
    cross_recv,
    fin_send,
    fin_recv,
):
    batch, rows, width = q_v.shape
    pages, _, page = kv_hbm.shape[1:]
    tokens = pages * page
    slots = slots_ref.shape[1]
    me = lax.axis_index("ctx")
    half = n // 2
    left = me < half
    inward = jnp.where(left, me + 1, me - 1)
    outward = jnp.where(left, me - 1, me + 1)
    is_end = (me == 0) | (me == n - 1)
    is_mid = (me == half - 1) | (me == half)
    inner = jnp.logical_not(is_end)

    loads = [pltpu.make_async_copy(q_hbm.at[0], q_v, load_sem.at[pages])]
    for i in range(pages):
        loads.append(
            pltpu.make_async_copy(
                kv_hbm.at[0, i],
                kv_v.at[:, pl.ds(i * page, page)],
                load_sem.at[i],
            )
        )
    for load in loads:
        load.start()

    barrier = pltpu.get_barrier_semaphore()

    @pl.loop(1, n)
    def _(off):
        pl.semaphore_signal(
            barrier, inc=1, device_id={"ctx": lax.rem(me + off, n)}, device_id_type=MESH
        )

    own_v[...] = jnp.zeros((page, width), jnp.bfloat16)
    own_v[0:batch, :] = latent_ref[0]

    slot_id = me * pages + lax.broadcasted_iota(jnp.int32, (pages, slots), 0)
    rank = lax.broadcasted_iota(jnp.int32, (pages, slots), 1)
    match = slots_ref[...] == slot_id
    lane = lax.broadcasted_iota(jnp.int32, (pages, page), 1)
    lane_own = lax.broadcasted_iota(jnp.int32, (8, page), 1)
    begin = jnp.int32(0)
    for s in range(batch):
        count = counts_ref[0, s]
        length = (count - 1) * page + tails_ref[0, s]
        place = rank - begin
        inside = match & (place >= 0) & (place < count)
        limit = jnp.sum(
            jnp.where(inside, (length - place * page).astype(jnp.float32), 0.0),
            axis=1,
            keepdims=True,
        )
        bias_v[s, 0:pages, :] = jnp.where(lane.astype(jnp.float32) < limit, 0.0, NEG)
        own_here = (lane_own == s) & (me == 0)
        bias_v[s, pages : pages + 8, :] = jnp.where(own_here, 0.0, NEG)
        begin = begin + count

    loads[0].wait()
    queries = q_v[...].reshape(batch * rows, width)
    tops = [jnp.full((rows, page), NEG, jnp.float32) for _ in range(batch)]
    nt = (((1,), (1,)), ((), ()))
    for first in [*range(0, pages, 2), pages]:
        many = min(2, pages - first) or 1
        if first < pages:
            for j in range(many):
                loads[1 + first + j].wait()
            keys = kv_v[:, first * page : (first + many) * page]
            block = jnp.dot(queries, keys, preferred_element_type=jnp.float32)
        else:
            block = lax.dot_general(
                queries, own_v[...], nt, preferred_element_type=jnp.float32
            )
        for s in range(batch):
            for j in range(many):
                at = first + j
                value = (
                    block[s * rows : (s + 1) * rows, j * page : (j + 1) * page] * SCALE
                    + bias_v[s, at : at + 1, :]
                )
                score_v[s, :, at * page : (at + 1) * page] = value
                tops[s] = jnp.maximum(tops[s], value)

    size = batch * rows // PIECES
    wide = out_ref.shape[3] // page

    def piece(k):
        return k // PIECES, pl.ds((k % PIECES) * size, size)

    def ship(source, target, send, recv, k, to):
        s, at = piece(k)
        return pltpu.make_async_remote_copy(
            src_ref=source.at[s, at],
            dst_ref=target.at[s, at],
            send_sem=send.at[k],
            recv_sem=recv.at[k],
            device_id={"ctx": to},
            device_id_type=MESH,
        )

    def stat_copy(s, to, origin, slot):
        return pltpu.make_async_remote_copy(
            src_ref=stat_out.at[s],
            dst_ref=stat_in.at[s, origin],
            send_sem=stat_send.at[s, slot],
            recv_sem=stat_recv.at[s, origin],
            device_id={"ctx": to},
            device_id_type=MESH,
        )

    def other(off):
        to = lax.rem(me + off, n)
        return to, (to > 0) & (to < n - 1)

    lane_row = lax.broadcasted_iota(jnp.int32, (rows, page), 1)
    for s in range(batch):
        top = jnp.max(tops[s], axis=1, keepdims=True)
        total = jnp.zeros((rows, page), jnp.float32)
        for at in range(pages + 1):
            cols = slice(at * page, (at + 1) * page)
            weight = jnp.exp2(score_v[s, :, cols] - top).astype(jnp.bfloat16)
            weight_v[s * rows : (s + 1) * rows, cols] = weight
            total = total + weight.astype(jnp.float32)
        total = jnp.sum(total, axis=1, keepdims=True)
        pair = jnp.where(lane_row == 0, top, total)
        square = jnp.concatenate([pair] * (page // rows), axis=0)
        tile = jnp.transpose(square)[0:8]
        stat_out[s] = tile
        stat_in[s, pl.ds(me, 1)] = tile[None]
        if s == 0:
            pl.semaphore_wait(barrier, n - 1)

        @pl.loop(1, n)
        def _(off):
            to, wanted = other(off)

            @pl.when(wanted)
            def _():
                stat_copy(s, to, me, off).start()

    group = 2
    for j in range(0, wide, group):
        span = slice(j * page, (j + group) * page)
        block = lax.dot_general(
            weight_v[:, 0:tokens], kv_v[span, :], nt, preferred_element_type=jnp.float32
        ) + jnp.dot(
            weight_v[:, tokens:], own_v[:, span], preferred_element_type=jnp.float32
        )
        for i in range(group):
            acc_v[j + i] = block[:, i * page : (i + 1) * page]

        @pl.when(is_end)
        def _():
            for k in range(j * PIECES, (j + group) * PIECES):
                ship(acc_v, inbox, in_send, in_recv, k, inward).start()

    def emit(k, value):
        j = k // PIECES
        first = (k % PIECES) * size
        value = value.astype(jnp.bfloat16)
        for lo in range(0, size, min(size, rows)):
            s, r = divmod(first + lo, rows)
            out_ref[0, s, r : r + min(size, rows), j * page : (j + 1) * page] = value[
                lo : lo + min(size, rows)
            ]

    number = wide * PIECES
    from_end = (outward == 0) | (outward == n - 1)

    def factors(s):
        @pl.loop(1, n)
        def _(off):
            stat_copy(s, me, lax.rem(me + off, n), off).wait_recv()

        best = stat_in[s, 0]
        for j in range(1, n):
            best = jnp.maximum(best, stat_in[s, j])
        best = best[0:1]
        denom = jnp.zeros((1, page), jnp.float32)
        mine = jnp.zeros((1, page), jnp.float32)
        theirs = jnp.zeros((1, page), jnp.float32)
        for j in range(n):
            tile = stat_in[s, j]
            keep = jnp.exp2(tile[0:1] - best)
            denom = denom + keep * tile[1:2]
            mine = jnp.where(me == j, keep, mine)
            theirs = jnp.where(outward == j, keep, theirs)
        mine = mine / denom
        theirs = jnp.where(from_end, theirs / denom, 1.0)
        row = lax.broadcasted_iota(jnp.int32, (page, page), 0)
        turned = jnp.transpose(jnp.where(row == 0, mine, theirs))
        return turned[0:rows, 0:1], turned[0:rows, 1:2]

    @pl.when(inner)
    def _():
        pairs = [factors(s) for s in range(batch)]
        scales = [jnp.concatenate(f, axis=0) for f in zip(*pairs)]
        for k in range(number + LAG):
            if k < number:
                s, at = piece(k)
                lo = (k % PIECES) * size
                mine, theirs = (f[lo : lo + size] for f in scales)
                ship(acc_v, inbox, in_send, in_recv, k, inward).wait_recv()
                part_v[s, at] = acc_v[s, at] * mine + inbox[s, at] * theirs

                @pl.when(is_mid)
                def _():
                    ship(part_v, cross, in_send, cross_recv, k, inward).start()

                @pl.when(jnp.logical_not(is_mid))
                def _():
                    ship(part_v, inbox, in_send, in_recv, k, inward).start()

            if k >= LAG:
                d = k - LAG
                s, at = piece(d)

                @pl.when(is_mid)
                def _():
                    ship(part_v, cross, in_send, cross_recv, d, inward).wait_recv()
                    total = part_v[s, at] + cross[s, at]
                    total_v[s, at] = total
                    ship(total_v, final, fin_send, fin_recv, d, outward).start()
                    emit(d, total)

                @pl.when(jnp.logical_not(is_mid))
                def _():
                    ship(final, final, fin_send, fin_recv, d, outward).wait_recv()
                    ship(final, final, fin_send, fin_recv, d, outward).start()
                    emit(d, final[s, at])

        for k in range(number):
            ship(total_v, final, fin_send, fin_recv, k, outward).wait_send()

    @pl.when(is_end)
    def _():
        for k in range(number):
            s, at = piece(k)
            ship(total_v, final, fin_send, fin_recv, k, inward).wait_recv()
            emit(k, final[s, at])

    for k in range(number):
        ship(part_v, inbox, in_send, in_recv, k, inward).wait_send()
    for s in range(batch):

        @pl.loop(1, n)
        def _(off):
            to, wanted = other(off)

            @pl.when(wanted)
            def _():
                stat_copy(s, to, me, off).wait_send()


def local(n, kv_cache, queries, new_latent, page_counts, page_tails, page_slots):
    _, pages, page, width = kv_cache.shape
    _, batch, rows, _ = queries.shape
    number = LATENT // page * PIECES
    block = (LATENT // page, batch * rows, page)
    vmem = pl.BlockSpec(memory_space=pltpu.VMEM)
    smem = pl.BlockSpec(memory_space=pltpu.SMEM)
    hbm = pl.BlockSpec(memory_space=pltpu.HBM)
    dma = pltpu.SemaphoreType.DMA
    return pl.pallas_call(
        functools.partial(kernel, n),
        out_shape=jax.ShapeDtypeStruct((1, batch, rows, LATENT), jnp.bfloat16),
        in_specs=[smem, smem, vmem, vmem, hbm, hbm],
        out_specs=vmem,
        scratch_shapes=[
            pltpu.VMEM((batch, rows, width), jnp.bfloat16),
            pltpu.VMEM((width, pages * page), jnp.bfloat16),
            pltpu.VMEM((page, width), jnp.bfloat16),
            pltpu.VMEM((batch, pages + 8, page), jnp.float32),
            pltpu.VMEM((batch, rows, (pages + 1) * page), jnp.float32),
            pltpu.VMEM((batch * rows, (pages + 1) * page), jnp.bfloat16),
            pltpu.VMEM(block, jnp.float32),
            pltpu.VMEM(block, jnp.float32),
            pltpu.VMEM(block, jnp.float32),
            pltpu.VMEM(block, jnp.float32),
            pltpu.VMEM(block, jnp.float32),
            pltpu.VMEM(block, jnp.float32),
            pltpu.VMEM((batch, 8, page), jnp.float32),
            pltpu.VMEM((batch, n, 8, page), jnp.float32),
            dma((pages + 1,)),
            dma((batch, n)),
            dma((batch, n)),
            dma((number,)),
            dma((number,)),
            dma((number,)),
            dma((number,)),
            dma((number,)),
        ],
        compiler_params=pltpu.CompilerParams(
            collective_id=0, has_side_effects=True
        ),
    )(page_counts, page_tails, page_slots, new_latent, queries, jnp.swapaxes(kv_cache, 2, 3))


def solution(mesh):
    in_specs = (
        P(("groups", "rep"), "ctx", None, None),
        P(("groups", "rep"), None, "head", None),
        P(("groups", "rep"), None, None),
        P(("groups", "rep"), None),
        P(("groups", "rep"), None),
        P(("groups", "rep"), None),
    )
    out_specs = P(("groups", "rep"), None, "head", None)
    return jax.shard_map(
        functools.partial(local, mesh.shape["ctx"]),
        mesh=mesh,
        in_specs=in_specs,
        out_specs=out_specs,
        check_vma=False,
    )
```

profile of v0, /device:TPU:0, one launch (start us, length us, event | category | flops | bytes accessed | tf_op | source)
XLA Modules:
  0.0 34.3 jit_solution(7368985828991238047)
XLA Ops:
  0.0 32.6 %shard_map.64 = bf16[1,4,64,512]{3,2,1,0:T(8,128)(2,1)} custom-call(s32[1,4]{1,0:T(1,128)} %counts_ref.1, s32[1,4]{1,0:T(1,128)} %tails_ref.1, s32[1,96]{1,0:T(1,128)} %slots_ref.1, bf16[1,4,576]{2,1,0:T(4,128)(2,1)} %latent_ref.1, bf16[1,4,64,576]{3,2,1,0:T(8,128)(2,1)} %q_hbm.1, bf16[1,24,576,128]{3,2,1,0:T(8,128)(2,1)} %bitcast.1), custom_call_target="tpu_custom_call" | custom-call | tf_op jit(solution)/shard_map/pallas_call | solution.py:313
  32.6 1.7 %copy.8 = bf16[1,4,64,512]{3,2,1,0:T(8,128)(2,1)} copy(bf16[1,4,64,512]{3,2,1,0:T(8,128)(2,1)} %shard_map.64) | data formatting | bytes 524288
where the time goes:
time: 34.5 us; the launch traced here: 34.3 us
  Pallas kernels  32.6 us (94%)
  local copies, waits for them, and re-layouts  1.67 us (5%)
    pallas_call x1, Pallas kernels, local(): pl.pallas_call(functools.partial(kernel, n), out_shape=jax.ShapeDtypeStru...  32.6 us
    unnamed x1, local copies, waits for them, and re-layouts  1.67 us

commit v1 on v0

--- a/solution.py
+++ b/solution.py
@@ -18,13 +18,17 @@
 
 def kernel(
     n,
+    counts_hbm,
+    tails_hbm,
+    slots_hbm,
+    latent_hbm,
+    q_hbm,
+    kv_hbm,
+    out_ref,
     counts_ref,
     tails_ref,
     slots_ref,
     latent_ref,
-    q_hbm,
-    kv_hbm,
-    out_ref,
     q_v,
     kv_v,
     own_v,
@@ -40,6 +44,7 @@
     stat_out,
     stat_in,
     load_sem,
+    small_sem,
     stat_send,
     stat_recv,
     in_send,
@@ -51,7 +56,7 @@
     batch, rows, width = q_v.shape
     pages, _, page = kv_hbm.shape[1:]
     tokens = pages * page
-    slots = slots_ref.shape[1]
+    slots = slots_hbm.shape[1]
     me = lax.axis_index("ctx")
     half = n // 2
     left = me < half
@@ -61,6 +66,19 @@
     is_mid = (me == half - 1) | (me == half)
     inner = jnp.logical_not(is_end)
 
+    smalls = [
+        pltpu.make_async_copy(source, target, small_sem.at[i])
+        for i, (source, target) in enumerate(
+            [
+                (counts_hbm, counts_ref),
+                (tails_hbm, tails_ref),
+                (slots_hbm, slots_ref),
+                (latent_hbm, latent_ref),
+            ]
+        )
+    ]
+    for small in smalls:
+        small.start()
     loads = [pltpu.make_async_copy(q_hbm.at[0], q_v, load_sem.at[pages])]
     for i in range(pages):
         loads.append(
@@ -81,6 +99,8 @@
             barrier, inc=1, device_id={"ctx": lax.rem(me + off, n)}, device_id_type=MESH
         )
 
+    for small in smalls:
+        small.wait()
     own_v[...] = jnp.zeros((page, width), jnp.bfloat16)
     own_v[0:batch, :] = latent_ref[0]
 
@@ -306,16 +326,17 @@
     _, batch, rows, _ = queries.shape
     number = LATENT // page * PIECES
     block = (LATENT // page, batch * rows, page)
-    vmem = pl.BlockSpec(memory_space=pltpu.VMEM)
-    smem = pl.BlockSpec(memory_space=pltpu.SMEM)
     hbm = pl.BlockSpec(memory_space=pltpu.HBM)
     dma = pltpu.SemaphoreType.DMA
     return pl.pallas_call(
         functools.partial(kernel, n),
-        out_shape=jax.ShapeDtypeStruct((1, batch, rows, LATENT), jnp.bfloat16),
-        in_specs=[smem, smem, vmem, vmem, hbm, hbm],
-        out_specs=vmem,
+        out_shape=pltpu.VMEM((1, batch, rows, LATENT), jnp.bfloat16),
+        in_specs=[hbm] * 6,
         scratch_shapes=[
+            pltpu.SMEM(page_counts.shape, jnp.int32),
+            pltpu.SMEM(page_tails.shape, jnp.int32),
+            pltpu.VMEM(page_slots.shape, jnp.int32),
+            pltpu.VMEM(new_latent.shape, jnp.bfloat16),
             pltpu.VMEM((batch, rows, width), jnp.bfloat16),
             pltpu.VMEM((width, pages * page), jnp.bfloat16),
             pltpu.VMEM((page, width), jnp.bfloat16),
@@ -331,6 +352,7 @@
             pltpu.VMEM((batch, 8, page), jnp.float32),
             pltpu.VMEM((batch, n, 8, page), jnp.float32),
             dma((pages + 1,)),
+            dma((4,)),
             dma((batch, n)),
             dma((batch, n)),
             dma((number,)),

time: 34.5 us -> 33 us (0.957)
  local copies, waits for them, and re-layouts: 1.67 us -> 0.71 us
  Pallas kernels: 32.6 us -> 32.1 us
    unnamed x1, local copies, waits for them, and re-layouts: 1.67 us -> 0.71 us
    pallas_call x1, Pallas kernels: 32.6 us -> 32.1 us  [local(): pl.pallas_call(functools.partial(kernel, n), out_shape=pltpu.VMEM((1, bat...]
where the time goes in v1:
time: 33 us; the launch traced here: 32.8 us
  Pallas kernels  32.1 us (97%)
  local copies, waits for them, and re-layouts  0.71 us (2%)
    pallas_call x1, Pallas kernels, local(): pl.pallas_call(functools.partial(kernel, n), out_shape=pltpu.VMEM((1, bat...  32.1 us
    unnamed x1, local copies, waits for them, and re-layouts  0.71 us

profile of v1, /device:TPU:0, one launch (start us, length us, event | category | flops | bytes accessed | tf_op | source)
XLA Modules:
  0.0 32.8 jit_solution(9283099174027648369)
XLA Ops:
  0.0 32.1 %shard_map.64 = bf16[1,4,64,512]{3,2,1,0:T(8,128)(2,1)S(1)} custom-call(s32[1,4]{1,0:T(1,128)} %counts_hbm.1, s32[1,4]{1,0:T(1,128)} %tails_hbm.1, s32[1,96]{1,0:T(1,128)} %slots_hbm.1, bf16[1,4,576]{2,1,0:T(4,128)(2,1)} %latent_hbm.1, bf16[1,4,64,576]{3,2,1,0:T(8,128)(2,1)} %q_hbm.1, bf16[1,24,576,128]{3,2,1,0:T(8,128)(2,1)} %bitcast.1), custom_call_target="tpu_custom_call" | custom-call | tf_op jit(solution)/shard_map/pallas_call | solution.py:331
  32.1 0.7 %copy.8 = bf16[1,4,64,512]{3,2,1,0:T(8,128)(2,1)} copy(bf16[1,4,64,512]{3,2,1,0:T(8,128)(2,1)S(1)} %shard_map.64) | data formatting | bytes 524288

commit v2 on v1

v2 whole, which is shorter than its diff:
```python
import functools
import math

import jax
import jax.numpy as jnp
from jax import lax
from jax.experimental import pallas as pl
from jax.experimental.pallas import tpu as pltpu
from jax.sharding import PartitionSpec as P

LATENT = 512
SCALE = 192.0 ** (-0.5) * math.log2(math.e)
NEG = -1e30
PIECE = 64
TAIL = ()
LAG = 6
CHUNKS = 1
MESH = pl.DeviceIdType.MESH


def cut(total):
    sizes = list(TAIL) if total > sum(TAIL) else []
    while sum(sizes) < total:
        sizes.insert(0, min(PIECE, total - sum(sizes)))
    return [(sum(sizes[:k]), size) for k, size in enumerate(sizes)]


def kernel(
    n,
    counts_hbm,
    tails_hbm,
    slots_hbm,
    latent_hbm,
    q_hbm,
    kv_hbm,
    out_ref,
    counts_ref,
    tails_ref,
    slots_ref,
    latent_ref,
    q_v,
    kv_v,
    own_v,
    bias_v,
    score_v,
    weight_v,
    acc_v,
    inbox,
    part_v,
    inner_box,
    total_v,
    stat_out,
    stat_in,
    small_sem,
    q_sem,
    kv_sem,
    stat_send,
    stat_recv,
    send_sem,
    out_recv,
    in_recv,
):
    batch, rows, width = q_v.shape
    pages, _, page = kv_v.shape
    tokens = pages * page
    slots = slots_ref.shape[1]
    height = batch * rows
    groups, many = stat_out.shape[0], page // rows
    wide = LATENT // page
    pieces = cut(wide * height)
    number = len(pieces)
    me = lax.axis_index("ctx")
    half = n // 2
    left = me < half
    inward = jnp.where(left, me + 1, me - 1)
    outward = jnp.where(left, me - 1, me + 1)
    is_end = (me == 0) | (me == n - 1)
    is_mid = (me == half - 1) | (me == half)
    inner = jnp.logical_not(is_end)
    all_mid = n <= 4

    smalls = [
        pltpu.make_async_copy(source, target, small_sem.at[i])
        for i, (source, target) in enumerate(
            [
                (counts_hbm, counts_ref),
                (tails_hbm, tails_ref),
                (slots_hbm, slots_ref),
                (latent_hbm, latent_ref),
            ]
        )
    ]
    for small in smalls:
        small.start()
    q_load = pltpu.make_async_copy(q_hbm.at[0], q_v, q_sem)
    q_load.start()
    step = pages // CHUNKS
    loads = []
    for i in range(CHUNKS):
        at = pl.ds(i * step, step)
        loads.append(
            pltpu.make_async_copy(kv_hbm.at[0, at], kv_v.at[at], kv_sem.at[i])
        )
        loads[-1].start(priority=1)

    barrier = pltpu.get_barrier_semaphore()

    @pl.loop(1, n)
    def _(off):
        pl.semaphore_signal(
            barrier, inc=1, device_id={"ctx": lax.rem(me + off, n)}, device_id_type=MESH
        )

    for small in smalls:
        small.wait()
    own_v[...] = jnp.zeros((page, width), jnp.bfloat16)
    own_v[0:batch, :] = latent_ref[0]

    slot_id = me * pages + lax.broadcasted_iota(jnp.int32, (pages, slots), 0)
    rank = lax.broadcasted_iota(jnp.int32, (pages, slots), 1)
    match = slots_ref[...] == slot_id
    lane = lax.broadcasted_iota(jnp.int32, (pages, page), 1)
    lane_own = lax.broadcasted_iota(jnp.int32, (8, page), 1)
    begin = jnp.int32(0)
    for s in range(batch):
        count = counts_ref[0, s]
        length = (count - 1) * page + tails_ref[0, s]
        place = rank - begin
        inside = match & (place >= 0) & (place < count)
        limit = jnp.sum(
            jnp.where(inside, (length - place * page).astype(jnp.float32), 0.0),
            axis=1,
            keepdims=True,
        )
        bias_v[s, 0:pages, :] = jnp.where(lane.astype(jnp.float32) < limit, 0.0, NEG)
        own_here = (lane_own == s) & (me == 0)
        bias_v[s, pages : pages + 8, :] = jnp.where(own_here, 0.0, NEG)
        begin = begin + count

    q_load.wait()
    queries = q_v[...].reshape(height, width)
    tops = [jnp.full((rows, page), NEG, jnp.float32) for _ in range(batch)]
    nt = (((1,), (1,)), ((), ()))
    for first in range(0, pages + 1, 2):
        two = min(2, pages + 1 - first)
        if first < pages:
            if first % step == 0:
                loads[first // step].wait()
            keys = jnp.concatenate([kv_v[first + j] for j in range(two)], axis=1)
            block = jnp.dot(queries, keys, preferred_element_type=jnp.float32)
        else:
            block = lax.dot_general(
                queries, own_v[...], nt, preferred_element_type=jnp.float32
            )
        for s in range(batch):
            for j in range(two):
                at = first + j
                value = (
                    block[s * rows : (s + 1) * rows, j * page : (j + 1) * page] * SCALE
                    + bias_v[s, at : at + 1, :]
                )
                score_v[at, s * rows : (s + 1) * rows, :] = value
                tops[s] = jnp.maximum(tops[s], value)

    tops = [jnp.max(top, axis=1, keepdims=True) for top in tops]
    totals = [jnp.zeros((rows, page), jnp.float32) for _ in range(batch)]
    for at in range(pages + 1):
        for s in range(batch):
            span = slice(s * rows, (s + 1) * rows)
            weight = jnp.exp2(score_v[at, span, :] - tops[s]).astype(jnp.bfloat16)
            weight_v[span, at * page : (at + 1) * page] = weight
            totals[s] = totals[s] + weight.astype(jnp.float32)

    def attend(first, blocks):
        span = slice(first * page, (first + blocks) * page)
        values = jnp.concatenate([kv_v[i, span, :] for i in range(pages)], axis=1)
        block = lax.dot_general(
            weight_v[:, 0:tokens], values, nt, preferred_element_type=jnp.float32
        ) + jnp.dot(
            weight_v[:, tokens:], own_v[:, span], preferred_element_type=jnp.float32
        )
        for i in range(blocks):
            acc_v[(first + i) * height : (first + i + 1) * height, :] = block[
                :, i * page : (i + 1) * page
            ]

    def ship(source, target, send, recv, k, to):
        at = pl.ds(*pieces[k])
        return pltpu.make_async_remote_copy(
            src_ref=source.at[at],
            dst_ref=target.at[at],
            send_sem=send_sem.at[send],
            recv_sem=recv.at[k],
            device_id={"ctx": to},
            device_id_type=MESH,
        )

    def to_inbox(source, k):
        return ship(source, inbox, 0, out_recv, k, inward)

    def to_mid(k):
        return ship(part_v, inner_box, 0, in_recv, k, inward)

    def to_out(source, k):
        return ship(source, inner_box, 1, in_recv, k, outward)

    def stat_copy(to, origin, slot):
        return pltpu.make_async_remote_copy(
            src_ref=stat_out,
            dst_ref=stat_in.at[origin],
            send_sem=stat_send.at[slot],
            recv_sem=stat_recv.at[origin],
            device_id={"ctx": to},
            device_id_type=MESH,
        )

    def other(off):
        to = lax.rem(me + off, n)
        return to, (to > 0) & (to < n - 1)

    lane_row = lax.broadcasted_iota(jnp.int32, (rows, page), 1)
    for g in range(groups):
        pairs = [
            jnp.where(lane_row == 0, tops[s], jnp.sum(totals[s], axis=1, keepdims=True))
            for s in range(g * many, (g + 1) * many)
        ]
        tile = jnp.transpose(jnp.concatenate(pairs, axis=0))[0:8]
        stat_out[g] = tile
        stat_in[pl.ds(me, 1), g] = tile[None]

    group = 2
    sent = 0
    for j in range(0, wide, group):
        attend(j, group)
        if j == 0:
            pl.semaphore_wait(barrier, n - 1)

            @pl.loop(1, n)
            def _(off):
                to, wanted = other(off)

                @pl.when(wanted)
                def _():
                    stat_copy(to, me, off).start()

        ready = [
            k for k in range(sent, number) if sum(pieces[k]) <= (j + group) * height
        ]
        sent += len(ready)

        @pl.when(is_end)
        def _():
            for k in ready:
                to_inbox(acc_v, k).start()

    def emit(k, value):
        value = value.astype(jnp.bfloat16)
        first, size = pieces[k]
        lo = first
        while lo < first + size:
            j, at = divmod(lo, height)
            s, r = divmod(at, rows)
            take = min(rows - r, first + size - lo)
            out_ref[0, s, r : r + take, j * page : (j + 1) * page] = value[
                lo - first : lo - first + take
            ]
            lo += take

    from_end = (outward == 0) | (outward == n - 1)

    def factors(g):
        best = stat_in[0, g]
        for j in range(1, n):
            best = jnp.maximum(best, stat_in[j, g])
        best = best[0:1]
        denom = jnp.zeros((1, page), jnp.float32)
        mine = jnp.zeros((1, page), jnp.float32)
        theirs = jnp.zeros((1, page), jnp.float32)
        for j in range(n):
            tile = stat_in[j, g]
            keep = jnp.exp2(tile[0:1] - best)
            denom = denom + keep * tile[1:2]
            mine = jnp.where(me == j, keep, mine)
            theirs = jnp.where(outward == j, keep, theirs)
        mine = mine / denom
        theirs = jnp.where(from_end, theirs / denom, 1.0)
        row = lax.broadcasted_iota(jnp.int32, (page, page), 0)
        turned = jnp.transpose(jnp.where(row == 0, mine, theirs))
        return turned[:, 0:1], turned[:, 1:2]

    def rows_of(factor, k):
        first, size = pieces[k]
        parts = []
        lo = first
        while lo < first + size:
            at = lo % height
            take = min(height - at, first + size - lo)
            parts.append(factor[at : at + take])
            lo += take
        return parts[0] if len(parts) == 1 else jnp.concatenate(parts, axis=0)

    @pl.when(inner)
    def _():
        @pl.loop(1, n)
        def _(off):
            stat_copy(me, lax.rem(me + off, n), off).wait_recv()

        pairs = [factors(g) for g in range(groups)]
        scales = [jnp.concatenate(f, axis=0) for f in zip(*pairs)]
        for k in range(number + LAG):
            if k < number:
                at = pl.ds(*pieces[k])
                mine, theirs = (rows_of(f, k) for f in scales)
                to_inbox(acc_v, k).wait_recv()
                part_v[at] = acc_v[at] * mine + inbox[at] * theirs
                if all_mid:
                    to_mid(k).start()
                else:

                    @pl.when(is_mid)
                    def _():
                        to_mid(k).start()

                    @pl.when(jnp.logical_not(is_mid))
                    def _():
                        to_inbox(part_v, k).start()

            if k >= LAG:
                d = k - LAG
                at = pl.ds(*pieces[d])
                to_mid(d).wait_recv()

                def finish():
                    total = part_v[at] + inner_box[at]
                    total_v[at] = total
                    to_out(total_v, d).start()
                    emit(d, total)

                if all_mid:
                    finish()
                else:
                    pl.when(is_mid)(finish)

                    @pl.when(jnp.logical_not(is_mid))
                    def _():
                        to_out(inner_box, d).start()
                        emit(d, inner_box[at])

        pltpu.make_async_remote_copy(
            src_ref=total_v,
            dst_ref=inner_box,
            send_sem=send_sem.at[1],
            recv_sem=in_recv.at[0],
            device_id={"ctx": outward},
            device_id_type=MESH,
        ).wait_send()

    @pl.when(is_end)
    def _():
        for k in range(number):
            to_mid(k).wait_recv()
            emit(k, inner_box[pl.ds(*pieces[k])])

    pltpu.make_async_remote_copy(
        src_ref=part_v,
        dst_ref=inbox,
        send_sem=send_sem.at[0],
        recv_sem=out_recv.at[0],
        device_id={"ctx": inward},
        device_id_type=MESH,
    ).wait_send()

    @pl.loop(1, n)
    def _(off):
        to, wanted = other(off)

        @pl.when(wanted)
        def _():
            stat_copy(to, me, off).wait_send()


def local(n, kv_cache, queries, new_latent, page_counts, page_tails, page_slots):
    _, pages, page, width = kv_cache.shape
    _, batch, rows, _ = queries.shape
    height = batch * rows
    flat = (LATENT // page * height, page)
    number = len(cut(flat[0]))
    groups = height // page
    hbm = pl.BlockSpec(memory_space=pltpu.HBM)
    dma = pltpu.SemaphoreType.DMA
    return pl.pallas_call(
        functools.partial(kernel, n),
        out_shape=pltpu.VMEM((1, batch, rows, LATENT), jnp.bfloat16),
        in_specs=[hbm] * 6,
        scratch_shapes=[
            pltpu.SMEM(page_counts.shape, jnp.int32),
            pltpu.SMEM(page_tails.shape, jnp.int32),
            pltpu.VMEM(page_slots.shape, jnp.int32),
            pltpu.VMEM(new_latent.shape, jnp.bfloat16),
            pltpu.VMEM((batch, rows, width), jnp.bfloat16),
            pltpu.VMEM((pages, width, page), jnp.bfloat16),
            pltpu.VMEM((page, width), jnp.bfloat16),
            pltpu.VMEM((batch, pages + 8, page), jnp.float32),
            pltpu.VMEM((pages + 1, height, page), jnp.float32),
            pltpu.VMEM((height, (pages + 1) * page), jnp.bfloat16),
            pltpu.VMEM(flat, jnp.float32),
            pltpu.VMEM(flat, jnp.float32),
            pltpu.VMEM(flat, jnp.float32),
            pltpu.VMEM(flat, jnp.float32),
            pltpu.VMEM(flat, jnp.float32),
            pltpu.VMEM((groups, 8, page), jnp.float32),
            pltpu.VMEM((n, groups, 8, page), jnp.float32),
            dma((4,)),
            dma,
            dma((CHUNKS,)),
            dma((n,)),
            dma((n,)),
            dma((2,)),
            dma((number,)),
            dma((number,)),
        ],
        compiler_params=pltpu.CompilerParams(
            collective_id=0, has_side_effects=True
        ),
    )(page_counts, page_tails, page_slots, new_latent, queries, jnp.swapaxes(kv_cache, 2, 3))


def solution(mesh):
    in_specs = (
        P(("groups", "rep"), "ctx", None, None),
        P(("groups", "rep"), None, "head", None),
        P(("groups", "rep"), None, None),
        P(("groups", "rep"), None),
        P(("groups", "rep"), None),
        P(("groups", "rep"), None),
    )
    out_specs = P(("groups", "rep"), None, "head", None)
    return jax.shard_map(
        functools.partial(local, mesh.shape["ctx"]),
        mesh=mesh,
        in_specs=in_specs,
        out_specs=out_specs,
        check_vma=False,
    )
```

time: 33 us -> 28.9 us (0.88)
  Pallas kernels: 32.1 us -> 28.1 us
    pallas_call x1, Pallas kernels: 32.1 us -> 28.1 us  [local(): pl.pallas_call(functools.partial(kernel, n), out_shape=pltpu.VMEM((1, bat...]
where the time goes in v2:
time: 28.9 us; the launch traced here: 28.8 us
  Pallas kernels  28.1 us (97%)
  local copies, waits for them, and re-layouts  0.71 us (2%)
    pallas_call x1, Pallas kernels, local(): pl.pallas_call(functools.partial(kernel, n), out_shape=pltpu.VMEM((1, bat...  28.1 us
    unnamed x1, local copies, waits for them, and re-layouts  0.71 us

profile of v2, /device:TPU:0, one launch (start us, length us, event | category | flops | bytes accessed | tf_op | source)
XLA Modules:
  0.0 28.8 jit_solution(6128989305526643833)
XLA Ops:
  0.0 28.1 %shard_map.64 = bf16[1,4,64,512]{3,2,1,0:T(8,128)(2,1)S(1)} custom-call(s32[1,4]{1,0:T(1,128)} %counts_hbm.1, s32[1,4]{1,0:T(1,128)} %tails_hbm.1, s32[1,96]{1,0:T(1,128)} %slots_hbm.1, bf16[1,4,576]{2,1,0:T(4,128)(2,1)} %latent_hbm.1, bf16[1,4,64,576]{3,2,1,0:T(8,128)(2,1)} %q_hbm.1, bf16[1,24,576,128]{3,2,1,0:T(8,128)(2,1)} %bitcast.1), custom_call_target="tpu_custom_call" | custom-call | tf_op jit(solution)/shard_map/pallas_call | solution.py:391
  28.1 0.7 %copy.8 = bf16[1,4,64,512]{3,2,1,0:T(8,128)(2,1)} copy(bf16[1,4,64,512]{3,2,1,0:T(8,128)(2,1)S(1)} %shard_map.64) | data formatting | bytes 524288

commit v3 on v2

--- a/solution.py
+++ b/solution.py
@@ -11,18 +11,32 @@
 LATENT = 512
 SCALE = 192.0 ** (-0.5) * math.log2(math.e)
 NEG = -1e30
-PIECE = 64
-TAIL = ()
-LAG = 6
-CHUNKS = 1
+PIECE = 32
+HEAD = ()
+LAG_LEFT = 320
+LAG_RIGHT = 320
+CHUNKS = 2
 MESH = pl.DeviceIdType.MESH
 
 
 def cut(total):
-    sizes = list(TAIL) if total > sum(TAIL) else []
+    sizes = list(HEAD) if total > sum(HEAD) else []
     while sum(sizes) < total:
-        sizes.insert(0, min(PIECE, total - sum(sizes)))
+        sizes.append(min(PIECE, total - sum(sizes)))
     return [(sum(sizes[:k]), size) for k, size in enumerate(sizes)]
+
+
+def merge(pieces, lag):
+    order = []
+    k = d = 0
+    while d < len(pieces):
+        if k < len(pieces) and pieces[k][0] < pieces[d][0] + lag:
+            order.append((k, None))
+            k += 1
+        else:
+            order.append((None, d))
+            d += 1
+    return order
 
 
 def kernel(
@@ -42,6 +56,8 @@
     kv_v,
     own_v,
     bias_v,
+    owner_v,
+    across_v,
     score_v,
     weight_v,
     acc_v,
@@ -120,8 +136,9 @@
     rank = lax.broadcasted_iota(jnp.int32, (pages, slots), 1)
     match = slots_ref[...] == slot_id
     lane = lax.broadcasted_iota(jnp.int32, (pages, page), 1)
-    lane_own = lax.broadcasted_iota(jnp.int32, (8, page), 1)
     begin = jnp.int32(0)
+    limits = jnp.zeros((pages, page), jnp.float32)
+    table = jnp.zeros((pages, page), jnp.float32)
     for s in range(batch):
         count = counts_ref[0, s]
         length = (count - 1) * page + tails_ref[0, s]
@@ -132,57 +149,102 @@
             axis=1,
             keepdims=True,
         )
-        bias_v[s, 0:pages, :] = jnp.where(lane.astype(jnp.float32) < limit, 0.0, NEG)
-        own_here = (lane_own == s) & (me == 0)
-        bias_v[s, pages : pages + 8, :] = jnp.where(own_here, 0.0, NEG)
+        limits = limits + limit
+        table = jnp.where(lane == s, limit, table)
+        owner_v[s, :, :] = jnp.where(limit > 0.0, jnp.ones((pages, page)), 0.0)
         begin = begin + count
+    bias_v[...] = jnp.where(lane.astype(jnp.float32) < limits, 0.0, NEG)
+    square = jnp.concatenate(
+        [table, jnp.zeros((page - pages, page), jnp.float32)], axis=0
+    )
+    across_v[...] = jnp.transpose(square)[0:8]
 
     q_load.wait()
     queries = q_v[...].reshape(height, width)
-    tops = [jnp.full((rows, page), NEG, jnp.float32) for _ in range(batch)]
+    column = lax.broadcasted_iota(jnp.int32, (rows, page), 1)
+    peaks = jnp.full((rows, page), NEG, jnp.float32)
     nt = (((1,), (1,)), ((), ()))
-    for first in range(0, pages + 1, 2):
-        two = min(2, pages + 1 - first)
-        if first < pages:
-            if first % step == 0:
-                loads[first // step].wait()
-            keys = jnp.concatenate([kv_v[first + j] for j in range(two)], axis=1)
-            block = jnp.dot(queries, keys, preferred_element_type=jnp.float32)
-        else:
-            block = lax.dot_general(
-                queries, own_v[...], nt, preferred_element_type=jnp.float32
+
+    def pick(at, parts):
+        chosen = parts[-1]
+        for s in reversed(range(batch - 1)):
+            chosen = jnp.where(owner_v[s, at : at + 1, :] > 0.5, parts[s], chosen)
+        return chosen
+
+    def strips_of(block, j):
+        cols = slice(j * page, (j + 1) * page)
+        return [block[s * rows : (s + 1) * rows, cols] for s in range(batch)]
+
+    block = lax.dot_general(queries, own_v[...], nt, preferred_element_type=jnp.float32)
+    owns = [
+        jnp.where((column == s) & (me == 0), strip * SCALE, NEG)
+        for s, strip in enumerate(strips_of(block, 0))
+    ]
+    for first in range(0, pages, 2):
+        two = min(2, pages - first)
+        if first % step == 0:
+            loads[first // step].wait()
+        keys = jnp.concatenate([kv_v[first + j] for j in range(two)], axis=1)
+        block = jnp.dot(queries, keys, preferred_element_type=jnp.float32)
+        for j in range(two):
+            at = first + j
+            value = pick(at, strips_of(block, j)) * SCALE + bias_v[at : at + 1, :]
+            score_v[at] = value
+            peaks = jnp.where(
+                column == at, jnp.max(value, axis=1, keepdims=True), peaks
             )
-        for s in range(batch):
-            for j in range(two):
-                at = first + j
-                value = (
-                    block[s * rows : (s + 1) * rows, j * page : (j + 1) * page] * SCALE
-                    + bias_v[s, at : at + 1, :]
-                )
-                score_v[at, s * rows : (s + 1) * rows, :] = value
-                tops[s] = jnp.maximum(tops[s], value)
-
-    tops = [jnp.max(top, axis=1, keepdims=True) for top in tops]
-    totals = [jnp.zeros((rows, page), jnp.float32) for _ in range(batch)]
-    for at in range(pages + 1):
-        for s in range(batch):
-            span = slice(s * rows, (s + 1) * rows)
-            weight = jnp.exp2(score_v[at, span, :] - tops[s]).astype(jnp.bfloat16)
-            weight_v[span, at * page : (at + 1) * page] = weight
-            totals[s] = totals[s] + weight.astype(jnp.float32)
-
-    def attend(first, blocks):
-        span = slice(first * page, (first + blocks) * page)
-        values = jnp.concatenate([kv_v[i, span, :] for i in range(pages)], axis=1)
-        block = lax.dot_general(
-            weight_v[:, 0:tokens], values, nt, preferred_element_type=jnp.float32
-        ) + jnp.dot(
-            weight_v[:, tokens:], own_v[:, span], preferred_element_type=jnp.float32
-        )
-        for i in range(blocks):
+
+    tops = []
+    for s in range(batch):
+        held = jnp.where(across_v[s : s + 1, :] > 0.0, peaks, NEG)
+        tops.append(jnp.max(jnp.maximum(held, owns[s]), axis=1, keepdims=True))
+    spread = [jnp.broadcast_to(top, (rows, page)) for top in tops]
+    sums = jnp.zeros((rows, page), jnp.float32)
+    tiles = [(at, min(2, pages - at)) for at in range(0, pages, 2)] + [(pages, 1)]
+    group = 2
+
+    def attend(weights, first, at, count):
+        span = slice(first * page, (first + group) * page)
+        if at == pages:
+            return jnp.dot(weights, own_v[:, span], preferred_element_type=jnp.float32)
+        values = jnp.concatenate([kv_v[at + i, span, :] for i in range(count)], axis=1)
+        return lax.dot_general(weights, values, nt, preferred_element_type=jnp.float32)
+
+    def keep(first, block):
+        for i in range(group):
             acc_v[(first + i) * height : (first + i + 1) * height, :] = block[
                 :, i * page : (i + 1) * page
             ]
+
+    block = None
+    for at, count in tiles:
+        if at == pages:
+            strip = [
+                jnp.exp2(own - top).astype(jnp.bfloat16)
+                for own, top in zip(owns, spread)
+            ]
+            owns = [part.astype(jnp.float32) for part in strip]
+            weights = jnp.concatenate(strip, axis=0)
+        else:
+            strips = []
+            for i in range(at, at + count):
+                weight = jnp.exp2(score_v[i] - pick(i, spread)).astype(jnp.bfloat16)
+                total = jnp.sum(weight.astype(jnp.float32), axis=1, keepdims=True)
+                sums = jnp.where(column == i, total, sums)
+                strip = [
+                    weight * owner_v[s, i : i + 1, :].astype(jnp.bfloat16)
+                    for s in range(batch)
+                ]
+                strips.append(jnp.concatenate(strip, axis=0))
+            weights = jnp.concatenate(strips, axis=1)
+        weight_v[:, at * page : (at + count) * page] = weights
+        more = attend(weights, 0, at, count)
+        block = more if block is None else block + more
+    totals = [
+        jnp.where(across_v[s : s + 1, :] > 0.0, sums, 0.0) + owns[s]
+        for s in range(batch)
+    ]
+    keep(0, block)
 
     def ship(source, target, send, recv, k, to):
         at = pl.ds(*pieces[k])
@@ -228,21 +290,25 @@
         stat_out[g] = tile
         stat_in[pl.ds(me, 1), g] = tile[None]
 
-    group = 2
+    pl.semaphore_wait(barrier, n - 1)
+
+    @pl.loop(1, n)
+    def _(off):
+        to, wanted = other(off)
+
+        @pl.when(wanted)
+        def _():
+            stat_copy(to, me, off).start()
+
     sent = 0
     for j in range(0, wide, group):
-        attend(j, group)
-        if j == 0:
-            pl.semaphore_wait(barrier, n - 1)
-
-            @pl.loop(1, n)
-            def _(off):
-                to, wanted = other(off)
-
-                @pl.when(wanted)
-                def _():
-                    stat_copy(to, me, off).start()
-
+        if j > 0:
+            block = None
+            for at, count in tiles:
+                weights = weight_v[:, at * page : (at + count) * page]
+                more = attend(weights, j, at, count)
+                block = more if block is None else block + more
+            keep(j, block)
         ready = [
             k for k in range(sent, number) if sum(pieces[k]) <= (j + group) * height
         ]
@@ -266,27 +332,45 @@
             ]
             lo += take
 
-    from_end = (outward == 0) | (outward == n - 1)
-
-    def factors(g):
-        best = stat_in[0, g]
-        for j in range(1, n):
-            best = jnp.maximum(best, stat_in[j, g])
-        best = best[0:1]
+    def beyond(dist):
+        return jnp.where(left, jnp.maximum(me - dist, 0), jnp.minimum(me + dist, n - 1))
+
+    def turn(first, second):
+        row = lax.broadcasted_iota(jnp.int32, (page, page), 0)
+        turned = jnp.transpose(jnp.where(row == 0, first, second))
+        return turned[:, 0:1], turned[:, 1:2]
+
+    def part_factors(g):
+        theirs = stat_in[pl.ds(beyond(1), 1), g, 0:1, :].reshape(1, page)
+        for dist in range(2, half):
+            theirs = jnp.maximum(
+                theirs, stat_in[pl.ds(beyond(dist), 1), g, 0:1, :].reshape(1, page)
+            )
+        mine = stat_out[g, 0:1, :]
+        best = jnp.maximum(mine, theirs)
+        return turn(jnp.exp2(mine - best), jnp.exp2(theirs - best))
+
+    def total_factors(g):
+        tiles = [stat_in[j, g] for j in range(n)]
+        low = functools.reduce(jnp.maximum, tiles[:half])[0:1]
+        high = functools.reduce(jnp.maximum, tiles[half:])[0:1]
+        best = jnp.maximum(low, high)
         denom = jnp.zeros((1, page), jnp.float32)
-        mine = jnp.zeros((1, page), jnp.float32)
-        theirs = jnp.zeros((1, page), jnp.float32)
-        for j in range(n):
-            tile = stat_in[j, g]
-            keep = jnp.exp2(tile[0:1] - best)
-            denom = denom + keep * tile[1:2]
-            mine = jnp.where(me == j, keep, mine)
-            theirs = jnp.where(outward == j, keep, theirs)
-        mine = mine / denom
-        theirs = jnp.where(from_end, theirs / denom, 1.0)
-        row = lax.broadcasted_iota(jnp.int32, (page, page), 0)
-        turned = jnp.transpose(jnp.where(row == 0, mine, theirs))
-        return turned[:, 0:1], turned[:, 1:2]
+        for tile in tiles:
+            denom = denom + jnp.exp2(tile[0:1] - best) * tile[1:2]
+        low = jnp.exp2(low - best) / denom
+        high = jnp.exp2(high - best) / denom
+        return turn(jnp.where(left, low, high), jnp.where(left, high, low))
+
+    def await_stats(wanted):
+        @pl.loop(1, n)
+        def _(off):
+            origin = lax.rem(me + off, n)
+            outer = jnp.where(left, origin < me, origin > me)
+
+            @pl.when(outer == wanted)
+            def _():
+                stat_copy(me, origin, off).wait_recv()
 
     def rows_of(factor, k):
         first, size = pieces[k]
@@ -301,50 +385,68 @@
 
     @pl.when(inner)
     def _():
-        @pl.loop(1, n)
-        def _(off):
-            stat_copy(me, lax.rem(me + off, n), off).wait_recv()
-
-        pairs = [factors(g) for g in range(groups)]
-        scales = [jnp.concatenate(f, axis=0) for f in zip(*pairs)]
-        for k in range(number + LAG):
-            if k < number:
-                at = pl.ds(*pieces[k])
-                mine, theirs = (rows_of(f, k) for f in scales)
-                to_inbox(acc_v, k).wait_recv()
-                part_v[at] = acc_v[at] * mine + inbox[at] * theirs
-                if all_mid:
-                    to_mid(k).start()
+        def scales(factors):
+            pairs = [factors(g) for g in range(groups)]
+            return [jnp.concatenate(f, axis=0) for f in zip(*pairs)]
+
+        await_stats(True)
+        part_scales = scales(part_factors)
+
+        def walk(lag):
+            total_scales = None
+            for k, d in merge(pieces, lag):
+                if k is not None:
+                    at = pl.ds(*pieces[k])
+                    mine, theirs = (rows_of(f, k) for f in part_scales)
+                    to_inbox(acc_v, k).wait_recv()
+                    part_v[at] = acc_v[at] * mine + inbox[at] * theirs
+                    if all_mid:
+                        to_mid(k).start()
+                    else:
+
+                        @pl.when(is_mid)
+                        def _():
+                            to_mid(k).start()
+
+                        @pl.when(jnp.logical_not(is_mid))
+                        def _():
+                            to_inbox(part_v, k).start()
+
                 else:
-
-                    @pl.when(is_mid)
-                    def _():
-                        to_mid(k).start()
-
-                    @pl.when(jnp.logical_not(is_mid))
-                    def _():
-                        to_inbox(part_v, k).start()
-
-            if k >= LAG:
-                d = k - LAG
-                at = pl.ds(*pieces[d])
-                to_mid(d).wait_recv()
-
-                def finish():
-                    total = part_v[at] + inner_box[at]
-                    total_v[at] = total
-                    to_out(total_v, d).start()
-                    emit(d, total)
-
-                if all_mid:
-                    finish()
-                else:
-                    pl.when(is_mid)(finish)
-
-                    @pl.when(jnp.logical_not(is_mid))
-                    def _():
-                        to_out(inner_box, d).start()
-                        emit(d, inner_box[at])
+                    at = pl.ds(*pieces[d])
+                    if total_scales is None:
+                        await_stats(False)
+                        total_scales = scales(total_factors)
+                    mine, theirs = (rows_of(f, d) for f in total_scales)
+                    to_mid(d).wait_recv()
+
+                    def finish():
+                        total = part_v[at] * mine + inner_box[at] * theirs
+                        total_v[at] = total
+                        to_out(total_v, d).start()
+                        emit(d, total)
+
+                    if all_mid:
+                        finish()
+                    else:
+                        pl.when(is_mid)(finish)
+
+                        @pl.when(jnp.logical_not(is_mid))
+                        def _():
+                            to_out(inner_box, d).start()
+                            emit(d, inner_box[at])
+
+        if LAG_LEFT == LAG_RIGHT:
+            walk(LAG_LEFT)
+        else:
+
+            @pl.when(left)
+            def _():
+                walk(LAG_LEFT)
+
+            @pl.when(jnp.logical_not(left))
+            def _():
+                walk(LAG_RIGHT)
 
         pltpu.make_async_remote_copy(
             src_ref=total_v,
@@ -400,8 +502,10 @@
             pltpu.VMEM((batch, rows, width), jnp.bfloat16),
             pltpu.VMEM((pages, width, page), jnp.bfloat16),
             pltpu.VMEM((page, width), jnp.bfloat16),
-            pltpu.VMEM((batch, pages + 8, page), jnp.float32),
-            pltpu.VMEM((pages + 1, height, page), jnp.float32),
+            pltpu.VMEM((pages, page), jnp.float32),
+            pltpu.VMEM((batch, pages, page), jnp.float32),
+            pltpu.VMEM((8, page), jnp.float32),
+            pltpu.VMEM((pages, rows, page), jnp.float32),
             pltpu.VMEM((height, (pages + 1) * page), jnp.bfloat16),
             pltpu.VMEM(flat, jnp.float32),
             pltpu.VMEM(flat, jnp.float32),

time: 28.9 us -> 28.1 us (0.972)
  Pallas kernels: 28.1 us -> 27.2 us
    pallas_call x1, Pallas kernels: 28.1 us -> 27.2 us  [local(): pl.pallas_call(functools.partial(kernel, n), out_shape=pltpu.VMEM((1, bat...]
where the time goes in v3:
time: 28.1 us; the launch traced here: 27.9 us
  Pallas kernels  27.2 us (97%)
  local copies, waits for them, and re-layouts  0.71 us (3%)
    pallas_call x1, Pallas kernels, local(): pl.pallas_call(functools.partial(kernel, n), out_shape=pltpu.VMEM((1, bat...  27.2 us
    unnamed x1, local copies, waits for them, and re-layouts  0.71 us

profile of v3, /device:TPU:0, one launch (start us, length us, event | category | flops | bytes accessed | tf_op | source)
XLA Modules:
  0.0 27.9 jit_solution(13282255243004358461)
XLA Ops:
  0.0 27.2 %shard_map.64 = bf16[1,4,64,512]{3,2,1,0:T(8,128)(2,1)S(1)} custom-call(s32[1,4]{1,0:T(1,128)} %counts_hbm.1, s32[1,4]{1,0:T(1,128)} %tails_hbm.1, s32[1,96]{1,0:T(1,128)} %slots_hbm.1, bf16[1,4,576]{2,1,0:T(4,128)(2,1)} %latent_hbm.1, bf16[1,4,64,576]{3,2,1,0:T(8,128)(2,1)} %q_hbm.1, bf16[1,24,576,128]{3,2,1,0:T(8,128)(2,1)} %bitcast.1), custom_call_target="tpu_custom_call" | custom-call | tf_op jit(solution)/shard_map/pallas_call | solution.py:493
  27.2 0.7 %copy.8 = bf16[1,4,64,512]{3,2,1,0:T(8,128)(2,1)} copy(bf16[1,4,64,512]{3,2,1,0:T(8,128)(2,1)S(1)} %shard_map.64) | data formatting | bytes 524288

commit v4 on v3

--- a/solution.py
+++ b/solution.py
@@ -11,18 +11,22 @@
 LATENT = 512
 SCALE = 192.0 ** (-0.5) * math.log2(math.e)
 NEG = -1e30
-PIECE = 32
-HEAD = ()
-LAG_LEFT = 320
-LAG_RIGHT = 320
+PIECE = 48
+HEAD = (16,16)
+TAIL = (16,16)
+LAG_LEFT = 304
+LAG_RIGHT = 352
 CHUNKS = 2
 MESH = pl.DeviceIdType.MESH
 
 
 def cut(total):
-    sizes = list(HEAD) if total > sum(HEAD) else []
-    while sum(sizes) < total:
-        sizes.append(min(PIECE, total - sum(sizes)))
+    ends = sum(HEAD) + sum(TAIL)
+    head, tail = (HEAD, TAIL) if total > ends else ((), ())
+    sizes = list(head)
+    while sum(sizes) + sum(tail) < total:
+        sizes.append(min(PIECE, total - sum(sizes) - sum(tail)))
+    sizes.extend(tail)
     return [(sum(sizes[:k]), size) for k, size in enumerate(sizes)]
 
 

time: 28.1 us -> 28.1 us (level)
  no operation moved by 1% of the time
where the time goes in v4:
time: 28.1 us; the launch traced here: 28 us
  Pallas kernels  27.3 us (97%)
  local copies, waits for them, and re-layouts  0.71 us (3%)
    pallas_call x1, Pallas kernels, local(): pl.pallas_call(functools.partial(kernel, n), out_shape=pltpu.VMEM((1, bat...  27.3 us
    unnamed x1, local copies, waits for them, and re-layouts  0.71 us

profile of v4, /device:TPU:0, one launch (start us, length us, event | category | flops | bytes accessed | tf_op | source)
XLA Modules:
  0.0 28.0 jit_solution(8286201688434385623)
XLA Ops:
  0.0 27.3 %shard_map.64 = bf16[1,4,64,512]{3,2,1,0:T(8,128)(2,1)S(1)} custom-call(s32[1,4]{1,0:T(1,128)} %counts_hbm.1, s32[1,4]{1,0:T(1,128)} %tails_hbm.1, s32[1,96]{1,0:T(1,128)} %slots_hbm.1, bf16[1,4,576]{2,1,0:T(4,128)(2,1)} %latent_hbm.1, bf16[1,4,64,576]{3,2,1,0:T(8,128)(2,1)} %q_hbm.1, bf16[1,24,576,128]{3,2,1,0:T(8,128)(2,1)} %bitcast.1), custom_call_target="tpu_custom_call" | custom-call | tf_op jit(solution)/shard_map/pallas_call | solution.py:497
  27.3 0.7 %copy.8 = bf16[1,4,64,512]{3,2,1,0:T(8,128)(2,1)} copy(bf16[1,4,64,512]{3,2,1,0:T(8,128)(2,1)S(1)} %shard_map.64) | data formatting | bytes 524288
